TPU v7x, 32 devices: a whole 2x2x4 slice. The times are simulated.
32 devices in a mesh: gx: 8 (over y, x, core), gy: 4 (over z).
Axes of the slice: x: 2, y: 2, z: 4, core: 2. Of those that a mesh axis runs over, the one named last changes fastest.
Arguments:
- features: bfloat16 [16384, 128], P(('gx', 'gy')), may hold values from -6 to 6
- cache_in: bfloat16 [16384, 128], replicated, may hold values from -26 to 26
- cache_hidden: bfloat16 [16384, 128], replicated, may hold values from -26 to 26
- tiles: bfloat16 [32, 32, 256, 256], P(('gx', 'gy')), may hold values from -0.0625 to 0.0625
- tile_pos: int32 [32, 32, 2], P(('gx', 'gy')), may hold values from 0 to 1
- order: int32 [2, 32], replicated, may hold values from 0 to 31, each once within a row
- skip: int32 [2, 32], replicated, may hold values 0 or 1
- w_first: bfloat16 [128, 128], replicated, may hold values from -0.5 to 0.5
- w_second: bfloat16 [128, 128], replicated, may hold values from -0.5 to 0.5
Outputs:
- output: bfloat16 [16384, 128], P(('gx', 'gy'))
- drift: float32 [2], replicated
Inputs may be any that keep to these rules, and one draw needn't show every extreme that they name: `order`: each row names every block once.
All inputs are finite; a program needn't handle non-finite values.
Results may differ from a plain program's by a relative error of at most 0.0052.
Values may be sent and summed in bfloat16 or wider, within the bound.
A program may use at most 192 MiB of HBM per device.

v0:
```python
import jax
import jax.numpy as jnp
from jax import lax
from jax.sharding import PartitionSpec as P


def refreshed_flags(order, skip):
    block_count = order.shape[1]
    round_hits = (
        order[:, :, None] == jnp.arange(block_count, dtype=jnp.int32)[None, None, :]
    ).astype(jnp.int32)
    return jnp.sum(round_hits * (1 - skip)[:, :, None], axis=1)


def make_fold(cached, fresh_flags, my_tiles, my_pos, own_index):
    tile_rows = my_tiles.shape[1]
    block_rows = 2 * tile_rows

    def fold_step(carry, piece, start):
        piece_blocks = piece.shape[0] // block_rows
        feat_width = piece.shape[1]
        new_blocks = piece.reshape(piece_blocks, 2, tile_rows, feat_width)
        old_blocks = cached.reshape(piece_blocks, 2, tile_rows, feat_width)
        block_ids = jnp.arange(piece_blocks, dtype=jnp.int32)
        use_new = (fresh_flags == 1) | (block_ids == own_index)
        source = jnp.where(use_new[:, None, None, None], new_blocks, old_blocks)
        halves = jnp.where((my_pos[:, 1] == 0)[:, None, None], source[:, 0], source[:, 1])
        products = jnp.einsum("kab,kbf->kaf", my_tiles, halves, preferred_element_type=jnp.float32)
        upper = (my_pos[:, 0] == 0)[:, None, None]
        upper_sum = jnp.sum(jnp.where(upper, products, jnp.float32(0.0)), axis=0)
        lower_sum = jnp.sum(jnp.where(upper, jnp.float32(0.0), products), axis=0)
        summed = jnp.concatenate([upper_sum, lower_sum], axis=0)
        drift_sum = carry[1]
        return (summed, drift_sum)

    return fold_step


def aggregate(block, cached, fresh_flags, my_tiles, my_pos, own_index):
    initial = (jnp.zeros(block.shape, jnp.float32), jnp.zeros((), jnp.float32))
    fold_step = make_fold(cached, fresh_flags, my_tiles, my_pos, own_index)
    column = lax.all_gather(block, "gy", axis=0, tiled=True)
    return fold_step(initial, lax.all_gather(column, "gx", axis=0, tiled=True), jnp.int32(0))


def owner_terms(block, cached, own_index):
    block_rows = block.shape[0]
    own_cache = lax.dynamic_slice_in_dim(cached, own_index * block_rows, block_rows, 0)
    change = block.astype(jnp.float32) - own_cache.astype(jnp.float32)
    return jnp.sum(change * change)


def drift_total(block, cached, own_index):
    return lax.psum(owner_terms(block, cached, own_index), ("gx", "gy"))


def on_device(features, cache_in, cache_hidden, tiles, tile_pos, order, skip, w_first, w_second):
    own_index = lax.axis_index(("gx", "gy"))
    fresh_flags = refreshed_flags(order, skip)
    my_tiles = tiles[0]
    my_pos = tile_pos[0]
    input_cells = cache_in.shape[0] * cache_in.shape[1]
    hidden_cells = cache_hidden.shape[0] * cache_hidden.shape[1]
    drift_input = drift_total(features, cache_in, own_index)
    first_sum, fold_first = aggregate(
        features, cache_in, fresh_flags[0], my_tiles, my_pos, own_index
    )
    first_agg = first_sum.astype(jnp.bfloat16)
    hidden = jnp.maximum(
        jnp.dot(first_agg, w_first, preferred_element_type=jnp.float32), 0.0
    ).astype(jnp.bfloat16)
    drift_hidden = drift_total(hidden, cache_hidden, own_index)
    second_sum, fold_second = aggregate(
        hidden, cache_hidden, fresh_flags[1], my_tiles, my_pos, own_index
    )
    output = jnp.dot(
        second_sum.astype(jnp.bfloat16), w_second, preferred_element_type=jnp.float32
    ).astype(jnp.bfloat16)
    drift = jnp.stack([drift_input / input_cells, drift_hidden / hidden_cells])
    return (output, drift)


def solution(mesh):
    in_specs = (
        P(("gx", "gy"), None),
        P(),
        P(),
        P(("gx", "gy"), None, None, None),
        P(("gx", "gy"), None, None),
        P(),
        P(),
        P(),
        P(),
    )
    out_specs = (P(("gx", "gy"), None), P())
    return jax.shard_map(
        on_device, mesh=mesh, in_specs=in_specs, out_specs=out_specs, check_vma=False
    )
```

profile of v0, /device:TPU:0, one launch (start us, length us, event | category | flops | bytes accessed | tf_op | source)
XLA Modules:
  0.0 164.2 jit_solution(9931714498727391533)
XLA Ops:
  7.2 0.0 copy-start
  7.2 0.0 all-gather.3.cloned.1.call-start
  7.2 19.3 %all_gather.12 = bf16[2048,128]{1,0:T(8,128)(2,1)} all-gather(bf16[512,128]{1,0:T(8,128)(2,1)} %param.9), channel_id=1, replica_groups=mesh['gx'=8,'gy'=4] {'gy'}, dimensions={0}, use_global_device_ids=true | all-gather | bytes 655360 | tf_op jit(solution)/shard_map/all_gather | solution.py:42
  26.6 0.0 all-gather.3.cloned.1.call-update
  26.6 0.0 all-gather.5.cloned.1.call-start
  26.7 6.4 %copy.16 = bf16[32,2,256,128]{2,3,0,1:T(8,128)(2,1)} copy(bf16[32,2,256,128]{3,2,1,0:T(8,128)(2,1)} %bitcast.66) | data formatting | bytes 8388608 | tf_op jit(solution)/shard_map/reshape | solution.py:23
  33.1 0.1 select_reduce_fusion.4
  33.2 29.9 %all-gather.3.cloned.1.call-done = bf16[16384,128]{1,0:T(8,128)(2,1)} async-done(((bf16[2048,128]{1,0:T(8,128)(2,1)}), bf16[16384,128]{1,0:T(8,128)(2,1)}) %all-gather.3.cloned.1.call-update) | async-done | bytes 4194320 | tf_op jit(solution)/shard_map/all_gather | solution.py:43
  63.1 6.4 %copy.15 = bf16[32,2,256,128]{2,3,0,1:T(8,128)(2,1)} copy(bf16[32,2,256,128]{3,2,1,0:T(8,128)(2,1)} %bitcast.68) | data formatting | bytes 8388608 | tf_op jit(solution)/shard_map/reshape | solution.py:22
  69.4 4.1 %broadcast_select_fusion = bf16[32,2,256,128]{2,3,0,1:T(8,128)(2,1)S(1)} fusion(bf16[32,2,256,128]{2,3,0,1:T(8,128)(2,1)} %copy.15, bf16[32,2,256,128]{2,3,0,1:T(8,128)(2,1)} %copy.16, pred[32]{0:T(512)(128)(4,1)S(1)} %get-tuple-element.9), kind=kLoop, calls=%fused_computation.8 | loop fusion | flops 2097152 | bytes 12582944 | tf_op jit(solution)/shard_map/jit(_where)/select_n | solution.py:26
  73.6 0.5 copy-done.6
  74.1 1.6 select_reduce_fusion.3
  75.7 1.8 %multiply_reduce_fusion = (f32[]{:T(128)}, bf16[512,128]{1,0:T(8,128)(2,1)S(1)}) fusion(bf16[16384,128]{1,0:T(8,128)(2,1)} %param.11, s32[]{:T(128)S(6)} %select_n.44, bf16[128,128]{1,0:T(8,128)(2,1)S(1)} %copy-done, bf16[256,128]{0,1:T(8,128)(2,1)S(1)} %bitcast.74, bf16[256,128]{0,1:T(8,128)(2,1)S(1)} %bitcast.73), kind=kOutput, calls=%fused_computation.21 | convolution fusion | flops 17498112 | bytes 425992 | tf_op jit(solution)/shard_map/dot_general | solution.py:70
  77.4 16.4 %all_gather.14 = bf16[2048,128]{1,0:T(8,128)(2,1)} all-gather(bf16[512,128]{1,0:T(8,128)(2,1)S(1)} %get-tuple-element.13), channel_id=1, replica_groups=mesh['gx'=8,'gy'=4] {'gy'}, dimensions={0}, use_global_device_ids=true | all-gather | bytes 655360 | tf_op jit(solution)/shard_map/all_gather | solution.py:42
  93.8 0.0 all-gather.5.cloned.1.call-update
  93.9 6.4 %copy.18 = bf16[32,2,256,128]{2,3,0,1:T(8,128)(2,1)} copy(bf16[32,2,256,128]{3,2,1,0:T(8,128)(2,1)} %bitcast.67) | data formatting | bytes 8388608 | tf_op jit(solution)/shard_map/reshape | solution.py:23
  100.3 1.6 multiply_reduce_fusion.1
  101.9 40.2 %all-reduce = (f32[]{:T(128)}, f32[]{:T(128)}) all-reduce(f32[]{:T(128)} %get-tuple-element.12, f32[]{:T(128)} %multiply_reduce_fusion.1), channel_id=1, replica_groups=mesh['gx'=8,'gy'=4] {'gx','gy'}, use_global_device_ids=true, to_apply=%region_8.9 | all-reduce | flops 2 | bytes 16 | tf_op jit(solution)/shard_map/psum | solution.py:54
  143.3 0.6 pad_maximum_fusion
  143.9 6.4 %copy.17 = bf16[32,2,256,128]{2,3,0,1:T(8,128)(2,1)} copy(bf16[32,2,256,128]{3,2,1,0:T(8,128)(2,1)} %bitcast.69) | data formatting | bytes 8388608 | tf_op jit(solution)/shard_map/reshape | solution.py:22
  150.3 4.1 %broadcast_select_fusion.1 = bf16[32,2,256,128]{2,3,0,1:T(8,128)(2,1)S(1)} fusion(bf16[32,2,256,128]{2,3,0,1:T(8,128)(2,1)} %copy.17, bf16[32,2,256,128]{2,3,0,1:T(8,128)(2,1)} %copy.18, pred[32]{0:T(512)(128)(4,1)S(1)} %get-tuple-element.8), kind=kLoop, calls=%fused_computation.9 | loop fusion | flops 2097152 | bytes 12582944 | tf_op jit(solution)/shard_map/jit(_where)/select_n | solution.py:26
  154.4 0.5 copy-done.7
  154.9 1.6 select_reduce_fusion.1
  156.5 0.9 convolution_convert_fusion
  (17 shorter events, 0.1 us)
Async XLA Ops:
  7.2 68.5 %copy-start = (bf16[128,128]{1,0:T(8,128)(2,1)S(1)}, bf16[128,128]{1,0:T(8,128)(2,1)}, u32[]{:S(2)}) copy-start(bf16[128,128]{1,0:T(8,128)(2,1)} %param.16) | copy-start | bytes 98308
  7.2 55.9 %all-gather.3.cloned.1.call-start = ((), (), s32[]{:S(2)}) async-start(), calls=%async_computation | async-start | bytes 4718592 | tf_op jit(solution)/shard_map/all_gather | solution.py:43
  26.6 117.3 %all-gather.5.cloned.1.call-start = ((), (), s32[]{:S(2)}) async-start(), calls=%async_computation.1 | async-start | bytes 4718592 | tf_op jit(solution)/shard_map/all_gather | solution.py:43
  26.6 6.4 %copy-start.4 = (s32[2,32]{1,0:T(2,128)S(1)}, s32[2,32]{1,0:T(2,128)}, u32[]{:S(2)}) copy-start(s32[2,32]{1,0:T(2,128)} %param.15) | copy-start | bytes 772
  26.7 6.4 %copy-start.3 = (s32[2,32]{1,0:T(2,128)S(1)}, s32[2,32]{1,0:T(2,128)}, u32[]{:S(2)}) copy-start(s32[2,32]{1,0:T(2,128)} %param.14) | copy-start | bytes 772
  26.7 6.5 %copy-start.5 = (s32[1,32,2]{1,2,0:T(2,128)S(1)}, s32[1,32,2]{1,2,0:T(2,128)}, u32[]{:S(2)}) copy-start(s32[1,32,2]{1,2,0:T(2,128)} %param.13) | copy-start | bytes 772
  69.4 4.6 %copy-start.6 = (bf16[1,32,256,256]{3,2,1,0:T(8,128)(2,1)S(1)}, bf16[1,32,256,256]{3,2,1,0:T(8,128)(2,1)}, u32[]{:S(2)}) copy-start(bf16[1,32,256,256]{3,2,1,0:T(8,128)(2,1)} %param.12) | copy-start | bytes 12582916
  93.8 6.5 %copy-start.1 = (bf16[512,128]{1,0:T(8,128)(2,1)S(1)}, bf16[512,128]{1,0:T(8,128)(2,1)}, u32[]{:S(2)}) copy-start(bf16[512,128]{1,0:T(8,128)(2,1)} %param.9) | copy-start | bytes 393220
  150.3 4.6 %copy-start.7 = (bf16[1,32,256,256]{3,2,1,0:T(8,128)(2,1)S(1)}, bf16[1,32,256,256]{3,2,1,0:T(8,128)(2,1)}, u32[]{:S(2)}) copy-start(bf16[1,32,256,256]{3,2,1,0:T(8,128)(2,1)} %param.12) | copy-start | bytes 12582916
  154.9 1.6 copy-start.2
Sparse Core Ops, SparseCore 0:
  26.7 36.3 all-gather.2
  94.0 37.7 all-gather.4
where the time goes:
time: 165 us; the launch traced here: 164 us
  blocking collectives  75.9 us (46%)
  waiting for transfers between devices  29.9 us (18%)
  local copies, waits for them, and re-layouts  26.6 us (16%)
  between operations  15.5 us (9%)
  other arithmetic  10.5 us (6%)
  matrix products  5.79 us (4%)
    psum x1, blocking collectives, drift_total(): return lax.psum(owner_terms(block, cached, own_index), ('gx', 'gy'))  40.2 us
    all_gather x2, blocking collectives, aggregate(): column = lax.all_gather(block, 'gy', axis=0, tiled=True)  35.7 us
    all_gather x2, waiting for transfers between devices, aggregate(): lax.all_gather(column, 'gx', axis=0, tiled=True)  29.9 us
    reshape x2, local copies, waits for them, and re-layouts, fold_step(): old_blocks = cached.reshape(piece_blocks, 2, tile_rows, feat_width)  12.8 us
    reshape x2, local copies, waits for them, and re-layouts, fold_step(): new_blocks = piece.reshape(piece_blocks, 2, tile_rows, feat_width)  12.7 us
    select_n x2, other arithmetic, fold_step(): source = jnp.where(use_new[:, None, None, None], new_blocks, old_blocks)  8.23 us
  transfers between devices with their start and end apart: 2, of which 1 were waited for; matrix products, arithmetic and copies ran while one was open for 9% of the time, Pallas kernels for 0%

commit v1 on v0

v1 whole, which is shorter than its diff:
```python
import functools

import jax
import jax.numpy as jnp
from jax import lax
from jax.experimental import pallas as pl
from jax.experimental.pallas import tpu as pltpu
from jax.sharding import PartitionSpec as P

GROUP = 4
CACHE_SLOTS = 16
MESH = pl.DeviceIdType.MESH


def flip(value, bits):
    bit = 1
    while bit <= bits:
        if bits & bit:
            value = value + bit - 2 * bit * ((value // bit) % 2)
        bit *= 2
    return value


def hop_bit(d, k):
    low = d & -d
    high = 1 << (d.bit_length() - 1)
    return low if k % 2 == 0 else high


def pick(i, values):
    chosen = values[0]
    for t in range(1, len(values)):
        chosen = jnp.where(i == t, values[t], chosen)
    return chosen


def arrival_order(planes, depth):
    slots = [(d, k) for d in range(planes) for k in range(depth)]
    return sorted(slots, key=lambda s: (bin(s[0]).count("1") + s[1], s[1], s[0]))


def kernel(planes, depth, code_ref, feat_ref, cache_a, cache_b, tiles_ref, w1_ref, w2_ref,
           out_ref, drift_ref, got_a, got_b, tiles_v, cached, acc, parts,
           send_sems, recv_sems, cache_sems, tile_sem, feat_sem):
    half = planes * depth
    blocks = 2 * half
    rows = feat_ref.shape[0]
    tile_rows = rows // 2
    width = feat_ref.shape[1]
    gx = lax.axis_index("gx")
    gz = lax.axis_index("gy")
    plane = gx // 2
    core = gx % 2

    def device(c, d, k):
        return (flip(plane, d) * 2 + flip(core, c), flip(gz, k))

    def block_of(slot):
        x, z = device(*slot)
        return x * depth + z

    def slot_id(c, d, k):
        return c * half + d * depth + k

    got = (got_a, got_b)
    caches = (cache_a, cache_b)

    feat_copy = pltpu.make_async_copy(feat_ref, got_a.at[0], feat_sem)
    feat_copy.start()

    peers = [(1, 0, 0)] + [(0, 0, k) for k in range(1, depth)]
    bit = 1
    while bit < planes:
        peers.append((0, bit, 0))
        bit *= 2
    barrier = pltpu.get_barrier_semaphore()
    for peer in peers:
        pl.semaphore_signal(barrier, inc=1, device_id=device(*peer), device_id_type=MESH)
    pl.semaphore_wait(barrier, len(peers))

    def remote(layer, src, dst, hop):
        return pltpu.make_async_remote_copy(
            src_ref=got[layer].at[slot_id(*src)],
            dst_ref=got[layer].at[slot_id(*dst)],
            send_sem=send_sems.at[layer, slot_id(*dst)],
            recv_sem=recv_sems.at[layer, slot_id(*dst)],
            device_id=device(*hop),
            device_id_type=MESH,
        )

    def forwards(layer, d, k):
        copies = []
        bit = 1
        while bit < planes:
            if not d & bit and hop_bit(d | bit, k) == bit:
                copies.append(remote(layer, (0, d, k), (0, d | bit, k), (0, bit, 0)))
            bit *= 2
        if d == 0 and k == 0:
            for far in range(1, depth):
                copies.append(remote(layer, (0, 0, 0), (0, 0, far), (0, 0, far)))
        copies.append(remote(layer, (0, d, k), (1, d, k), (1, 0, 0)))
        return copies

    def wait_slot(layer, slot):
        remote(layer, slot, slot, (1, 0, 0)).wait_recv()

    order = arrival_order(planes, depth)
    groups = [order[i:i + GROUP] for i in range(0, half, GROUP)]
    folds = []
    for g, group in enumerate(groups):
        fold = [(0, d, k) for d, k in group]
        if g:
            fold = [(1, d, k) for d, k in groups[g - 1]] + fold
        folds.append(fold)
    folds.append([(1, d, k) for d, k in groups[-1]])
    uses = [(layer, slot) for layer in range(2) for fold in folds for slot in fold]

    def cache_copy(u):
        layer, slot = uses[u]
        start = pl.multiple_of(block_of(slot) * rows, rows)
        return pltpu.make_async_copy(
            caches[layer].at[pl.ds(start, rows)],
            cached.at[u % CACHE_SLOTS],
            cache_sems.at[u % CACHE_SLOTS],
        )

    def fold_slots(layer, fold, first_use):
        slot_values = [jnp.int32(slot_id(*s)) for s in fold]
        block_values = [block_of(s) for s in fold]

        def body(i, carry):
            s = pick(i, slot_values)
            j = pick(i, block_values)
            code = code_ref[layer, j]
            new = got[layer][s]
            old = cached[(first_use + i) % CACHE_SLOTS]
            change = new.astype(jnp.float32) - old.astype(jnp.float32)
            change = change * change
            parts[layer, j] = jnp.sum(change.reshape(rows // 8, 8, width), axis=0)
            source = lax.select(code >= 4, new, old)
            chosen = lax.select((code // 2) % 2 == 0, source[:tile_rows], source[tile_rows:])
            zeros = jnp.zeros_like(chosen)
            upper = code % 2 == 0
            spread = jnp.concatenate(
                [lax.select(upper, chosen, zeros), lax.select(upper, zeros, chosen)], axis=1
            )
            acc[...] += jnp.dot(tiles_v[j], spread, preferred_element_type=jnp.float32)
            return carry

        lax.fori_loop(0, len(fold), body, 0)

    use = 0
    tile_copy = pltpu.make_async_copy(tiles_ref.at[0], tiles_v, tile_sem)
    sent = []
    for layer in range(2):
        weight = (w1_ref, w2_ref)[layer]
        if layer == 0:
            feat_copy.wait()
        for g, fold in enumerate(folds):
            if g < len(groups):
                for d, k in groups[g]:
                    if (d, k) != (0, 0):
                        wait_slot(layer, (0, d, k))
                    for copy in forwards(layer, d, k):
                        copy.start()
                        sent.append(copy)
                    if layer == 0 and (d, k) == (0, 0):
                        tile_copy.start()
                        for u in range(min(CACHE_SLOTS, len(uses))):
                            cache_copy(u).start()
                        acc[...] = jnp.zeros_like(acc)
            if layer == 0 and g == 0:
                tile_copy.wait()
            for t, slot in enumerate(fold):
                if slot[0] == 1:
                    wait_slot(layer, slot)
                cache_copy(use + t).wait()
            fold_slots(layer, fold, use)
            for t in range(len(fold)):
                if use + t + CACHE_SLOTS < len(uses):
                    cache_copy(use + t + CACHE_SLOTS).start()
            use += len(fold)
        for part in range(2):
            agg = acc[:, part * width:(part + 1) * width].astype(jnp.bfloat16)
            mixed = jnp.dot(agg, weight[...], preferred_element_type=jnp.float32)
            place = pl.ds(part * tile_rows, tile_rows)
            if layer == 0:
                got_b[0, place] = jnp.maximum(mixed, 0.0).astype(jnp.bfloat16)
            else:
                out_ref[place] = mixed.astype(jnp.bfloat16)
        if layer == 0:
            acc[...] = jnp.zeros_like(acc)
    for layer in range(2):
        total = jnp.sum(jnp.sum(parts[layer], axis=0))
        drift_ref[layer] = total / (blocks * rows * width)
    for copy in sent:
        copy.wait_send()


def on_device(planes, depth, features, cache_in, cache_hidden, tiles, tile_pos, order, skip, w_first, w_second):
    own_index = lax.axis_index(("gx", "gy"))
    block_count = order.shape[1]
    rows, width = features.shape
    tile_rows = tiles.shape[2]
    ids = jnp.arange(block_count, dtype=jnp.int32)
    hits = order[:, :, None] == ids[None, None, :]
    fresh = jnp.sum(jnp.where(hits, (1 - skip)[:, :, None], 0), axis=1)
    fresh = jnp.where(ids[None, :] == own_index, 1, fresh)
    code = fresh * 4 + (tile_pos[0, :, 1] * 2 + tile_pos[0, :, 0])[None, :]
    vmem = pl.BlockSpec(memory_space=pltpu.VMEM)
    smem = pl.BlockSpec(memory_space=pltpu.SMEM)
    anywhere = pl.BlockSpec(memory_space=pl.ANY)
    return pl.pallas_call(
        functools.partial(kernel, planes, depth),
        out_shape=(
            jax.ShapeDtypeStruct((rows, width), jnp.bfloat16),
            jax.ShapeDtypeStruct((2,), jnp.float32),
        ),
        in_specs=[smem, anywhere, anywhere, anywhere, anywhere, vmem, vmem],
        out_specs=(vmem, smem),
        scratch_shapes=[
            pltpu.VMEM((block_count, rows, width), jnp.bfloat16),
            pltpu.VMEM((block_count, rows, width), jnp.bfloat16),
            pltpu.VMEM((block_count, tile_rows, tile_rows), jnp.bfloat16),
            pltpu.VMEM((CACHE_SLOTS, rows, width), jnp.bfloat16),
            pltpu.VMEM((tile_rows, 2 * width), jnp.float32),
            pltpu.VMEM((2, block_count, 8, width), jnp.float32),
            pltpu.SemaphoreType.DMA((2, block_count)),
            pltpu.SemaphoreType.DMA((2, block_count)),
            pltpu.SemaphoreType.DMA((CACHE_SLOTS,)),
            pltpu.SemaphoreType.DMA,
            pltpu.SemaphoreType.DMA,
        ],
        compiler_params=pltpu.CompilerParams(
            collective_id=0, has_side_effects=True, vmem_limit_bytes=60 * 1024 * 1024
        ),
    )(code, features, cache_in, cache_hidden, tiles, w_first, w_second)


def solution(mesh):
    in_specs = (
        P(("gx", "gy"), None),
        P(),
        P(),
        P(("gx", "gy"), None, None, None),
        P(("gx", "gy"), None, None),
        P(),
        P(),
        P(),
        P(),
    )
    out_specs = (P(("gx", "gy"), None), P())
    body = functools.partial(on_device, mesh.shape["gx"] // 2, mesh.shape["gy"])
    return jax.shard_map(body, mesh=mesh, in_specs=in_specs, out_specs=out_specs, check_vma=False)
```

time: 165 us -> 75.6 us (0.46)
  blocking collectives: 75.9 us -> 0 us
  Pallas kernels: 0 us -> 69.3 us
  waiting for transfers between devices: 29.9 us -> 0 us
  local copies, waits for them, and re-layouts: 26.6 us -> 2.68 us
  between operations: 15.5 us -> 0.65 us
  other arithmetic: 10.5 us -> 2.79 us
  matrix products: 5.79 us -> 0 us
    pallas_call x0 -> x1, Pallas kernels: none -> 69.3 us  [on_device(): pl.pallas_call(functools.partial(kernel, planes, depth), out_shape=(jax.S...]
    psum x1 -> x0, blocking collectives: 40.2 us -> none  [drift_total(): return lax.psum(owner_terms(block, cached, own_index), ('gx', 'gy'))]
    all_gather x2 -> x0, blocking collectives: 35.7 us -> none  [aggregate(): column = lax.all_gather(block, 'gy', axis=0, tiled=True)]
    all_gather x2 -> x0, waiting for transfers between devices: 29.9 us -> none  [aggregate(): lax.all_gather(column, 'gx', axis=0, tiled=True)]
    reshape x4 -> x0, local copies, waits for them, and re-layouts: 25.6 us -> none  [the longest x2 12.8 us: fold_step(): old_blocks = cached.reshape(piece_blocks, 2, tile_rows, feat_width)]
    select_n x2 -> x0, other arithmetic: 8.23 us -> none  [fold_step(): source = jnp.where(use_new[:, None, None, None], new_blocks, old_blocks)]
    dot_general x4 -> x0, matrix products: 5.79 us -> none  [the longest x2 3.16 us: fold_step(): jnp.einsum('kab,kbf->kaf', my_tiles, halves, preferred_element_type=jnp.f...]
  transfers between devices with their start and end apart: 2 -> 0, of which waited for: 1 -> 0; matrix products, arithmetic and copies ran while one was open for 9% -> 0% of each run, Pallas kernels for 0% -> 0%
where the time goes in v1:
time: 75.6 us; the launch traced here: 75.4 us
  Pallas kernels  69.3 us (92%)
  other arithmetic  2.79 us (4%)
  local copies, waits for them, and re-layouts  2.68 us (4%)
    pallas_call x1, Pallas kernels, on_device(): pl.pallas_call(functools.partial(kernel, planes, depth), out_shape=(jax.S...  69.3 us
    unnamed x2, local copies, waits for them, and re-layouts  2.68 us

profile of v1, /device:TPU:0, one launch (start us, length us, event | category | flops | bytes accessed | tf_op | source)
XLA Modules:
  0.0 75.4 jit_solution(13936102350649371015)
XLA Ops:
  0.6 0.8 %add_bitcast_fusion = s32[32]{0:T(128)S(1)} fusion(s32[1,32,2]{1,2,0:T(2,128)} %param.13), kind=kLoop, calls=%fused_computation.3 | loop fusion | flops 64 | bytes 384 | tf_op jit(solution)/shard_map/add | solution.py:209
  1.4 0.7 broadcast_subtract_fusion
  2.1 0.8 %select_reduce_fusion = s32[2,32]{1,0:T(2,128)S(1)} fusion(s32[2,32]{1,0:T(2,128)S(1)} %broadcast_subtract_fusion, s32[2,32]{1,0:T(2,128)} %param.14), kind=kLoop, calls=%fused_computation | loop fusion | flops 6080 | bytes 768 | tf_op jit(solution)/shard_map/reduce_sum | solution.py:207
  2.9 0.6 multiply_add_fusion.code_ref
  3.4 69.3 %shard_map.104 = (bf16[512,128]{1,0:T(8,128)(2,1)}, f32[2]{0:T(128)}) custom-call(s32[2,32]{1,0:T(2,128)} %multiply_add_fusion.code_ref, bf16[512,128]{1,0:T(8,128)(2,1)} %feat_ref.1, bf16[16384,128]{1,0:T(8,128)(2,1)} %cache_a.1, bf16[16384,128]{1,0:T(8,128)(2,1)} %cache_b.1, bf16[1,32,256,256]{3,2,1,0:T(8,128)(2,1)} %tiles_ref.1, bf16[128,128]{1,0:T(8,128)(2,1)} %w1_ref.1, ...), custom_call_target="tpu_custom_call" | custom-call | tf_op jit(solution)/shard_map/pallas_call | solution.py:213
  72.7 1.6 %copy.13 = bf16[512,128]{1,0:T(8,128)(2,1)} copy(bf16[512,128]{1,0:T(8,128)(2,1)} %get-tuple-element.4) | data formatting | bytes 262144
  74.3 1.1 %copy.14 = f32[2]{0:T(128)} copy(f32[2]{0:T(128)} %get-tuple-element.5) | data formatting | bytes 16
  (1 shorter events, 0.0 us)

commit v2 on v1

--- a/solution.py
+++ b/solution.py
@@ -9,6 +9,11 @@
 
 GROUP = 4
 CACHE_SLOTS = 16
+CHUNKS = 2
+COLUMN_COST = 2
+PLANE_COST = 3
+CHUNK_COST = 1
+COLUMN_SHARE = 2
 MESH = pl.DeviceIdType.MESH
 
 
@@ -21,10 +26,14 @@
     return value
 
 
-def hop_bit(d, k):
+def hop_bit(d, part):
     low = d & -d
     high = 1 << (d.bit_length() - 1)
-    return low if k % 2 == 0 else high
+    return low if part % 2 == 0 else high
+
+
+def by_column(d, k, part):
+    return d & (d - 1) != 0 and 0 < k * CHUNKS + part < COLUMN_SHARE + CHUNKS and k > 0
 
 
 def pick(i, values):
@@ -35,8 +44,13 @@
 
 
 def arrival_order(planes, depth):
-    slots = [(d, k) for d in range(planes) for k in range(depth)]
-    return sorted(slots, key=lambda s: (bin(s[0]).count("1") + s[1], s[1], s[0]))
+    events = [(d, k, h) for d in range(planes) for k in range(depth) for h in range(CHUNKS)]
+
+    def expected(event):
+        d, k, h = event
+        return (COLUMN_COST * k + PLANE_COST * bin(d).count("1") + CHUNK_COST * h, k, d, h)
+
+    return sorted(events, key=expected)
 
 
 def kernel(planes, depth, code_ref, feat_ref, cache_a, cache_b, tiles_ref, w1_ref, w2_ref,
@@ -78,41 +92,53 @@
         pl.semaphore_signal(barrier, inc=1, device_id=device(*peer), device_id_type=MESH)
     pl.semaphore_wait(barrier, len(peers))
 
-    def remote(layer, src, dst, hop):
+    piece = rows // CHUNKS
+
+    def remote(layer, src, dst, h, hop):
+        place = pl.ds(h * piece, piece)
+        sem = slot_id(*dst) * CHUNKS + h
         return pltpu.make_async_remote_copy(
-            src_ref=got[layer].at[slot_id(*src)],
-            dst_ref=got[layer].at[slot_id(*dst)],
-            send_sem=send_sems.at[layer, slot_id(*dst)],
-            recv_sem=recv_sems.at[layer, slot_id(*dst)],
+            src_ref=got[layer].at[slot_id(*src), place],
+            dst_ref=got[layer].at[slot_id(*dst), place],
+            send_sem=send_sems.at[layer, sem],
+            recv_sem=recv_sems.at[layer, sem],
             device_id=device(*hop),
             device_id_type=MESH,
         )
 
-    def forwards(layer, d, k):
+    def forwards(layer, d, k, h):
         copies = []
         bit = 1
         while bit < planes:
-            if not d & bit and hop_bit(d | bit, k) == bit:
-                copies.append(remote(layer, (0, d, k), (0, d | bit, k), (0, bit, 0)))
+            wider = d | bit
+            if wider != d and hop_bit(wider, k + h) == bit and not by_column(wider, k, h):
+                copies.append(remote(layer, (0, d, k), (0, d | bit, k), h, (0, bit, 0)))
             bit *= 2
-        if d == 0 and k == 0:
+        if k == 0:
             for far in range(1, depth):
-                copies.append(remote(layer, (0, 0, 0), (0, 0, far), (0, 0, far)))
-        copies.append(remote(layer, (0, d, k), (1, d, k), (1, 0, 0)))
+                if d == 0 or by_column(d, far, h):
+                    copies.append(remote(layer, (0, d, 0), (0, d, far), h, (0, 0, far)))
+        copies.append(remote(layer, (0, d, k), (1, d, k), h, (1, 0, 0)))
         return copies
 
-    def wait_slot(layer, slot):
-        remote(layer, slot, slot, (1, 0, 0)).wait_recv()
+    def wait_piece(layer, slot, h):
+        remote(layer, slot, slot, h, (1, 0, 0)).wait_recv()
 
     order = arrival_order(planes, depth)
-    groups = [order[i:i + GROUP] for i in range(0, half, GROUP)]
+    size = GROUP * CHUNKS
+    groups = [order[i:i + size] for i in range(0, len(order), size)]
+    done = []
     folds = []
-    for g, group in enumerate(groups):
-        fold = [(0, d, k) for d, k in group]
-        if g:
-            fold = [(1, d, k) for d, k in groups[g - 1]] + fold
-        folds.append(fold)
-    folds.append([(1, d, k) for d, k in groups[-1]])
+    waiting = []
+    for group in groups:
+        ready = []
+        for d, k, h in group:
+            done.append((d, k))
+            if done.count((d, k)) == CHUNKS:
+                ready.append((d, k))
+        folds.append([(1, d, k) for d, k in waiting] + [(0, d, k) for d, k in ready])
+        waiting = ready
+    folds.append([(1, d, k) for d, k in waiting])
     uses = [(layer, slot) for layer in range(2) for fold in folds for slot in fold]
 
     def cache_copy(u):
@@ -158,13 +184,13 @@
             feat_copy.wait()
         for g, fold in enumerate(folds):
             if g < len(groups):
-                for d, k in groups[g]:
+                for d, k, h in groups[g]:
                     if (d, k) != (0, 0):
-                        wait_slot(layer, (0, d, k))
-                    for copy in forwards(layer, d, k):
+                        wait_piece(layer, (0, d, k), h)
+                    for copy in forwards(layer, d, k, h):
                         copy.start()
                         sent.append(copy)
-                    if layer == 0 and (d, k) == (0, 0):
+                    if layer == 0 and (d, k, h) == (0, 0, 0):
                         tile_copy.start()
                         for u in range(min(CACHE_SLOTS, len(uses))):
                             cache_copy(u).start()
@@ -173,7 +199,8 @@
                 tile_copy.wait()
             for t, slot in enumerate(fold):
                 if slot[0] == 1:
-                    wait_slot(layer, slot)
+                    for h in range(CHUNKS):
+                        wait_piece(layer, slot, h)
                 cache_copy(use + t).wait()
             fold_slots(layer, fold, use)
             for t in range(len(fold)):
@@ -225,8 +252,8 @@
             pltpu.VMEM((CACHE_SLOTS, rows, width), jnp.bfloat16),
             pltpu.VMEM((tile_rows, 2 * width), jnp.float32),
             pltpu.VMEM((2, block_count, 8, width), jnp.float32),
-            pltpu.SemaphoreType.DMA((2, block_count)),
-            pltpu.SemaphoreType.DMA((2, block_count)),
+            pltpu.SemaphoreType.DMA((2, block_count * CHUNKS)),
+            pltpu.SemaphoreType.DMA((2, block_count * CHUNKS)),
             pltpu.SemaphoreType.DMA((CACHE_SLOTS,)),
             pltpu.SemaphoreType.DMA,
             pltpu.SemaphoreType.DMA,

time: 75.6 us -> 66.5 us (0.88)
  Pallas kernels: 69.3 us -> 60.1 us
    pallas_call x1, Pallas kernels: 69.3 us -> 60.1 us  [on_device(): pl.pallas_call(functools.partial(kernel, planes, depth), out_shape=(jax.S...]
where the time goes in v2:
time: 66.5 us; the launch traced here: 66.2 us
  Pallas kernels  60.1 us (90%)
  other arithmetic  2.79 us (4%)
  local copies, waits for them, and re-layouts  2.68 us (4%)
    pallas_call x1, Pallas kernels, on_device(): pl.pallas_call(functools.partial(kernel, planes, depth), out_shape=(jax.S...  60.1 us
    unnamed x2, local copies, waits for them, and re-layouts  2.68 us
    add x2, other arithmetic, on_device(): code = fresh * 4 + (tile_pos[0, :, 1] * 2 + tile_pos[0, :, 0])[None, :]  1.34 us

profile of v2, /device:TPU:0, one launch (start us, length us, event | category | flops | bytes accessed | tf_op | source)
XLA Modules:
  0.0 66.2 jit_solution(15832758564237068946)
XLA Ops:
  0.6 0.8 %add_bitcast_fusion = s32[32]{0:T(128)S(1)} fusion(s32[1,32,2]{1,2,0:T(2,128)} %param.13), kind=kLoop, calls=%fused_computation.3 | loop fusion | flops 64 | bytes 384 | tf_op jit(solution)/shard_map/add | solution.py:236
  1.4 0.7 %broadcast_subtract_fusion = s32[2,32]{1,0:T(2,128)S(1)} fusion(s32[2,32]{1,0:T(2,128)} %param.15), kind=kLoop, calls=%fused_computation.4 | loop fusion | flops 64 | bytes 512 | tf_op jit(solution)/shard_map/sub | solution.py:234
  2.1 0.8 %select_reduce_fusion = s32[2,32]{1,0:T(2,128)S(1)} fusion(s32[2,32]{1,0:T(2,128)S(1)} %broadcast_subtract_fusion, s32[2,32]{1,0:T(2,128)} %param.14), kind=kLoop, calls=%fused_computation | loop fusion | flops 6080 | bytes 768 | tf_op jit(solution)/shard_map/reduce_sum | solution.py:234
  2.9 0.6 multiply_add_fusion.code_ref
  3.4 60.1 %shard_map.104 = (bf16[512,128]{1,0:T(8,128)(2,1)}, f32[2]{0:T(128)}) custom-call(s32[2,32]{1,0:T(2,128)} %multiply_add_fusion.code_ref, bf16[512,128]{1,0:T(8,128)(2,1)} %feat_ref.1, bf16[16384,128]{1,0:T(8,128)(2,1)} %cache_a.1, bf16[16384,128]{1,0:T(8,128)(2,1)} %cache_b.1, bf16[1,32,256,256]{3,2,1,0:T(8,128)(2,1)} %tiles_ref.1, bf16[128,128]{1,0:T(8,128)(2,1)} %w1_ref.1, ...), custom_call_target="tpu_custom_call" | custom-call | tf_op jit(solution)/shard_map/pallas_call | solution.py:240
  63.6 1.6 %copy.13 = bf16[512,128]{1,0:T(8,128)(2,1)} copy(bf16[512,128]{1,0:T(8,128)(2,1)} %get-tuple-element.4) | data formatting | bytes 262144
  65.1 1.1 %copy.14 = f32[2]{0:T(128)} copy(f32[2]{0:T(128)} %get-tuple-element.5) | data formatting | bytes 16
  (1 shorter events, 0.0 us)

commit v3 on v2

--- a/solution.py
+++ b/solution.py
@@ -231,7 +231,7 @@
     tile_rows = tiles.shape[2]
     ids = jnp.arange(block_count, dtype=jnp.int32)
     hits = order[:, :, None] == ids[None, None, :]
-    fresh = jnp.sum(jnp.where(hits, (1 - skip)[:, :, None], 0), axis=1)
+    fresh = 1 - jnp.sum(jnp.where(hits, skip[:, :, None], 0), axis=1)
     fresh = jnp.where(ids[None, :] == own_index, 1, fresh)
     code = fresh * 4 + (tile_pos[0, :, 1] * 2 + tile_pos[0, :, 0])[None, :]
     vmem = pl.BlockSpec(memory_space=pltpu.VMEM)

time: 66.5 us -> 65.8 us (0.989)
    sub x1 -> x0, other arithmetic: 0.68 us -> none  [on_device(): fresh = jnp.sum(jnp.where(hits, (1 - skip)[:, :, None], 0), axis=1)]
where the time goes in v3:
time: 65.8 us; the launch traced here: 65.6 us
  Pallas kernels  60.1 us (91%)
  local copies, waits for them, and re-layouts  2.68 us (4%)
  other arithmetic  2.13 us (3%)
    pallas_call x1, Pallas kernels, on_device(): pl.pallas_call(functools.partial(kernel, planes, depth), out_shape=(jax.S...  60.1 us
    unnamed x2, local copies, waits for them, and re-layouts  2.68 us
    add x2, other arithmetic, on_device(): code = fresh * 4 + (tile_pos[0, :, 1] * 2 + tile_pos[0, :, 0])[None, :]  1.34 us

profile of v3, /device:TPU:0, one launch (start us, length us, event | category | flops | bytes accessed | tf_op | source)
XLA Modules:
  0.0 65.6 jit_solution(6031589788836240136)
XLA Ops:
  0.6 0.8 %add_bitcast_fusion = s32[32]{0:T(128)S(1)} fusion(s32[1,32,2]{1,2,0:T(2,128)} %param.13), kind=kLoop, calls=%fused_computation.3 | loop fusion | flops 64 | bytes 384 | tf_op jit(solution)/shard_map/add | solution.py:236
  1.4 0.8 %select_reduce_fusion = s32[2,32]{1,0:T(2,128)S(1)} fusion(s32[2,32]{1,0:T(2,128)} %param.15, s32[2,32]{1,0:T(2,128)} %param.14), kind=kLoop, calls=%fused_computation | loop fusion | flops 6080 | bytes 768 | tf_op jit(solution)/shard_map/reduce_sum | solution.py:234
  2.2 0.6 multiply_add_fusion.code_ref
  2.8 60.1 %shard_map.104 = (bf16[512,128]{1,0:T(8,128)(2,1)}, f32[2]{0:T(128)}) custom-call(s32[2,32]{1,0:T(2,128)} %multiply_add_fusion.code_ref, bf16[512,128]{1,0:T(8,128)(2,1)} %feat_ref.1, bf16[16384,128]{1,0:T(8,128)(2,1)} %cache_a.1, bf16[16384,128]{1,0:T(8,128)(2,1)} %cache_b.1, bf16[1,32,256,256]{3,2,1,0:T(8,128)(2,1)} %tiles_ref.1, bf16[128,128]{1,0:T(8,128)(2,1)} %w1_ref.1, ...), custom_call_target="tpu_custom_call" | custom-call | tf_op jit(solution)/shard_map/pallas_call | solution.py:240
  62.9 1.6 %copy.13 = bf16[512,128]{1,0:T(8,128)(2,1)} copy(bf16[512,128]{1,0:T(8,128)(2,1)} %get-tuple-element.4) | data formatting | bytes 262144
  64.5 1.1 %copy.14 = f32[2]{0:T(128)} copy(f32[2]{0:T(128)} %get-tuple-element.5) | data formatting | bytes 16
  (1 shorter events, 0.0 us)
